TPU v7x, 32 devices: a whole 2x2x4 slice. The times are simulated.
32 devices in a mesh: row: 8 (over z, x), col: 4 (over y, core).
Axes of the slice: x: 2, y: 2, z: 4, core: 2. Of those that a mesh axis runs over, the one named last changes fastest.
Arguments:
- gradients: bfloat16 [32, 2, 524288], P(('row', 'col')), may hold values from -96 to 96
- master_params: float32 [2, 524288], P(None, ('row', 'col')), may hold values from -0.1 to 0.1
- first_moment: float32 [2, 524288], P(None, ('row', 'col')), may hold values from -3 to 3
- second_moment: float32 [2, 524288], P(None, ('row', 'col')), may hold values from 0.05 to 5
Outputs:
- new_master: float32 [2, 524288], P(None, ('row', 'col'))
- new_first: float32 [2, 524288], P(None, ('row', 'col'))
- new_second: float32 [2, 524288], P(None, ('row', 'col'))
- new_weights: bfloat16 [2, 524288], replicated
All inputs are finite; a program needn't handle non-finite values.
Results may differ from a plain program's by a relative error of at most 0.009.
Values may be sent and summed in bfloat16 or wider, within the bound.
No kernel may reach another device: no remote copies, remote signals or barrier semaphores. Data moves between devices by JAX's collectives and lax.ppermute only.
A program may use at most 64 MiB of HBM per device.

v0:
```python
import jax
import jax.numpy as jnp
from jax import lax
from jax.experimental import pallas as pl
from jax.experimental.pallas import tpu as pltpu
from jax.sharding import PartitionSpec as P

beta_one = 0.9
beta_two = 0.95
learn_rate = 0.001
decay_rate = 0.1
epsilon = 1e-08
adam_step = 10.0

AXES = ("row", "col")
LANES = 128
Y, X, Z = 0, 1, 2
SHARES = (0, 8)
GATHER_GRANT = 52 << 20
SUM_ORDERS = (((X, Y, Z), (Y, Z, X)), ((X, Y, Z), (Z, X, Y)))
SPREAD_ORDERS = (((X, Z, Y), (Y, X, Z)), ((Y, X, Z), (Z, Y, X)))


def adam_update(mean_grad, master_params, first_moment, second_moment):
    new_first = beta_one * first_moment + (1.0 - beta_one) * mean_grad
    new_second = beta_two * second_moment + (1.0 - beta_two) * mean_grad * mean_grad
    first_hat = new_first / (1.0 - beta_one**adam_step)
    second_hat = new_second / (1.0 - beta_two**adam_step)
    new_master = master_params - learn_rate * (
        first_hat / (jnp.sqrt(second_hat) + epsilon) + decay_rate * master_params
    )
    return (new_master, new_first, new_second)


def rows_view(x):
    layers, n = x.shape
    return x.reshape(layers, n // LANES, LANES).transpose(1, 0, 2).reshape(-1, LANES)


def layers_view(x, layers):
    return x.reshape(-1, layers, LANES).transpose(1, 0, 2).reshape(layers, -1)


class Part:
    def __init__(self, low, high, orders):
        self.low, self.high, self.orders = low, high, orders
        self.size = high - low
        self.steps = len(orders[0])
        self.blocks = 1 << self.steps

    def mask(self, team, step):
        return 1 << self.orders[team][step] | 1

    def offset(self, team, position):
        bits = 0
        for step in range(self.steps):
            if position >> (self.steps - 1 - step) & 1:
                bits ^= self.mask(team, step)
        return bits


def parts_of(bits, rows, orders):
    rest = list(range(1, bits))
    if bits < 4:
        return [Part(0, rows, (rest, rest[::-1]))]
    tail = rest[3:]
    cuts = [8 * (rows * share // (8 * 16)) for share in SHARES] + [rows]
    return [
        Part(cuts[k], cuts[k + 1], [[rest[i] for i in order] + tail for order in orders[k]])
        for k in range(len(SHARES))
    ]


def place_index():
    devices = lax.axis_size("row") * lax.axis_size("col")
    me = lax.axis_index("row") * lax.axis_size("col") + lax.axis_index("col")
    team = me
    for bit in range(1, devices.bit_length() - 1):
        team = team ^ (me >> bit)
    return me, team & 1


def piece_of(part, me, team, mine, position):
    first, second = part.offset(0, position), part.offset(1, position)
    if not mine:
        first, second = second, first
    return (me if mine else me ^ 1) ^ jnp.where(team == 0, first, second)


def copy_all(pairs, sems):
    copies = [pltpu.make_async_copy(*pair, sems.at[n]) for n, pair in enumerate(pairs)]
    for copy in copies:
        copy.start()
    for copy in copies:
        copy.wait()


def rows_of(part, piece, rows):
    return pl.ds(pl.multiple_of(piece * rows + part.low, 8), part.size)


def gather_pieces(flat, parts, rows, base, grant):
    def body(flat_ref, *refs):
        me, team = place_index()
        pairs = []
        for n, part in enumerate(parts):
            for slot, mine in enumerate((False, True)):
                for k in range(part.blocks // 2):
                    piece = piece_of(part, me, team, mine, base + k)
                    src = flat_ref.at[rows_of(part, piece, rows), :]
                    pairs.append((src, refs[2 * n + slot].at[k]))
        copy_all(pairs, refs[-1])

    outs = [
        jax.ShapeDtypeStruct((part.blocks // 2, part.size, LANES), flat.dtype)
        for part in parts
        for _ in range(2)
    ]
    flat_outs = pl.pallas_call(
        body,
        out_shape=outs,
        in_specs=[pl.BlockSpec(memory_space=pl.ANY)],
        out_specs=[pl.BlockSpec(memory_space=pltpu.VMEM)] * len(outs),
        scratch_shapes=[pltpu.SemaphoreType.DMA((sum(part.blocks for part in parts),))],
        compiler_params=pltpu.CompilerParams(vmem_limit_bytes=grant),
        cost_estimate=pl.CostEstimate(flops=1 << 20, bytes_accessed=1 << 20, transcendentals=0),
        name="gather_pieces",
    )(flat)
    return [flat_outs[2 * n : 2 * n + 2] for n in range(len(parts))]


def scatter_pieces(whole, items, rows, total):
    def body(*refs):
        me, team = place_index()
        pairs = []
        for n, (part, mine, base, held) in enumerate(items):
            for k in range(held.shape[0]):
                piece = piece_of(part, me, team, mine, base + k)
                pairs.append((refs[n].at[k], refs[-2].at[rows_of(part, piece, rows), :]))
        copy_all(pairs, refs[-1])

    blocks = [held for _, _, _, held in items]
    in_specs = [pl.BlockSpec(memory_space=pltpu.VMEM)] * len(blocks)
    args, aliases = blocks, {}
    if whole is not None:
        in_specs.append(pl.BlockSpec(memory_space=pl.ANY))
        aliases = {len(blocks): 0}
        args = blocks + [whole]
    return pl.pallas_call(
        body,
        out_shape=jax.ShapeDtypeStruct((total, LANES), blocks[0].dtype),
        in_specs=in_specs,
        out_specs=pl.BlockSpec(memory_space=pl.ANY),
        scratch_shapes=[pltpu.SemaphoreType.DMA((sum(x.shape[0] for x in blocks),))],
        input_output_aliases=aliases,
        compiler_params=pltpu.CompilerParams(vmem_limit_bytes=8 << 20),
        cost_estimate=pl.CostEstimate(flops=1 << 20, bytes_accessed=1 << 20, transcendentals=0),
        name="scatter_pieces",
    )(*args)


def shards(gradients, master_params, first_moment, second_moment):
    devices = lax.axis_size("row") * lax.axis_size("col")
    layers = gradients.shape[1]
    bits = devices.bit_length() - 1
    flat = rows_view(gradients[0])
    rows = flat.shape[0] // devices
    parts = parts_of(bits, rows, SUM_ORDERS)
    routes = parts_of(bits, rows, SPREAD_ORDERS)

    def swap_cores(x):
        return lax.ppermute(x, AXES, [(i, i ^ 1) for i in range(devices)])

    def swap_chips(x, part, step):
        team = [i.bit_count() & 1 for i in range(devices)]
        return lax.ppermute(x, AXES, [(i, i ^ part.mask(team[i], step)) for i in range(devices)])

    def wide(x):
        return x.astype(jnp.float32)

    def narrow(x):
        return x.astype(jnp.bfloat16)

    upper = parts[0].blocks // 2
    highs = []
    for give, keep in gather_pieces(flat, parts, rows, upper, GATHER_GRANT):
        highs.append(narrow(wide(keep) + wide(swap_cores(give))))
    kept = []
    lows = gather_pieces(flat, parts, rows, 0, GATHER_GRANT)
    for n, (give, keep) in enumerate(lows):
        kept.append([highs[n], wide(keep) + wide(swap_cores(give))])
    sums = [None] * len(parts)
    for n, part in enumerate(parts):
        high, low = kept[n]
        for step in range(part.steps):
            came = wide(swap_chips(narrow(high), part, step))
            half = low.shape[0] // 2
            if half == 0:
                sums[n] = (low + came)[0]
            else:
                high = low[half:] + came[half:]
                low = low[:half] + came[:half]

    state = [rows_view(x) for x in (master_params, first_moment, second_moment)]
    held = []
    for n, part in enumerate(routes):
        new = adam_update(sums[n] / devices, *(x[part.low : part.high] for x in state))
        block = narrow(new[0])[None]
        for step in range(part.steps - 1, 0, -1):
            came = swap_chips(block, part, step)
            block = jnp.concatenate([block, came], axis=0)
        held.append(block)
    outs = adam_update(jnp.concatenate(sums, axis=0) / devices, *state)
    total = devices * rows
    early = [(p, True, 0, x) for p, x in zip(routes, held)]
    early += [(p, False, 0, swap_cores(x)) for p, x in zip(routes, held)]
    new_weights = scatter_pieces(None, early, rows, total)
    for n, part in enumerate(routes):
        high = swap_chips(held[n], part, 0)
        if n == 0:
            high, outs = lax.optimization_barrier((high, outs))
        other = swap_cores(high)
        late = [(part, True, upper, high), (part, False, upper, other)]
        new_weights = scatter_pieces(new_weights, late, rows, total)
    return tuple(layers_view(x, layers) for x in (*outs, new_weights))


def solution(mesh):
    in_specs = (P(AXES, None, None), P(None, AXES), P(None, AXES), P(None, AXES))
    out_specs = (P(None, AXES), P(None, AXES), P(None, AXES), P())
    return jax.shard_map(shards, mesh=mesh, in_specs=in_specs, out_specs=out_specs, check_vma=False)
```

profile of v0, /device:TPU:0, one launch (start us, length us, event | category | flops | bytes accessed | tf_op | source)
XLA Modules:
  0.0 53.9 jit_solution(32260879755954077)
XLA Ops:
  0.7 1.5 %gather_pieces.3 = (bf16[8,128,128]{2,1,0:T(8,128)(2,1)S(1)}, bf16[8,128,128]{2,1,0:T(8,128)(2,1)S(1)}, bf16[8,128,128]{2,1,0:T(8,128)(2,1)S(1)}, bf16[8,128,128]{2,1,0:T(8,128)(2,1)S(1)}) custom-call(bf16[8192,128]{1,0:T(8,128)(2,1)} %bitcast.114), custom_call_target="tpu_custom_call" | custom-call | flops 1048576 | bytes 1048576 | tf_op jit(solution)/shard_map/gather_pieces/pallas_call | solution.py:119
  2.2 0.6 %collective-permute-start.11 = (bf16[8,128,128]{2,1,0:T(8,128)(2,1)S(1)}, bf16[8,128,128]{2,1,0:T(8,128)(2,1)S(1)}, u32[]{:S(2)}, u32[]{:S(2)}) collective-permute-start(bf16[8,128,128]{2,1,0:T(8,128)(2,1)S(1)} %get-tuple-element.23), channel_id=1, source_target_pairs={{0,1},{1,0},{2,3},{3,2},{4,5},{5,4},{6,7},{7,6},{8,9},{9,8},{10,11... | collective-permute-start | bytes 786440 | tf_op jit(solution)/shard_map/ppermute | solution.py:172
  2.8 1.4 %gather_pieces.2 = (bf16[8,128,128]{2,1,0:T(8,128)(2,1)S(1)}, bf16[8,128,128]{2,1,0:T(8,128)(2,1)S(1)}, bf16[8,128,128]{2,1,0:T(8,128)(2,1)S(1)}, bf16[8,128,128]{2,1,0:T(8,128)(2,1)S(1)}) custom-call(bf16[8192,128]{1,0:T(8,128)(2,1)} %bitcast.115), custom_call_target="tpu_custom_call" | custom-call | flops 1048576 | bytes 1048576 | tf_op jit(solution)/shard_map/gather_pieces/pallas_call | solution.py:119
  5.1 2.7 %collective-permute-start.12 = (bf16[8,128,128]{2,1,0:T(8,128)(2,1)S(1)}, bf16[8,128,128]{2,1,0:T(8,128)(2,1)S(1)}, u32[]{:S(2)}, u32[]{:S(2)}) collective-permute-start(bf16[8,128,128]{2,1,0:T(8,128)(2,1)S(1)} %add_convert_fusion), channel_id=1, source_target_pairs={{0,5},{1,8},{2,11},{3,6},{4,13},{5,0},{6,3},{7,14},{8,1},{9,12},{1... | collective-permute-start | bytes 786440 | tf_op jit(solution)/shard_map/ppermute | solution.py:176
  7.9 1.4 %collective-permute-start.2 = (bf16[8,128,128]{2,1,0:T(8,128)(2,1)S(1)}, bf16[8,128,128]{2,1,0:T(8,128)(2,1)S(1)}, u32[]{:S(2)}, u32[]{:S(2)}) collective-permute-start(bf16[8,128,128]{2,1,0:T(8,128)(2,1)S(1)} %add_convert_fusion.1), channel_id=1, source_target_pairs={{0,5},{1,2},{2,1},{3,6},{4,7},{5,0},{6,3},{7,4},{8,11},{9,12},{10,... | collective-permute-start | bytes 786440 | tf_op jit(solution)/shard_map/ppermute | solution.py:176
  9.4 2.4 %collective-permute-done.12 = bf16[8,128,128]{2,1,0:T(8,128)(2,1)S(1)} collective-permute-done((bf16[8,128,128]{2,1,0:T(8,128)(2,1)S(1)}, bf16[8,128,128]{2,1,0:T(8,128)(2,1)S(1)}, u32[]{:S(2)}, u32[]{:S(2)}) %collective-permute-start.12) | collective-permute-done | bytes 262176 | tf_op jit(solution)/shard_map/ppermute | solution.py:176
  11.9 2.1 %collective-permute-start.13 = (bf16[4,128,128]{2,1,0:T(8,128)(2,1)S(1)}, bf16[4,128,128]{2,1,0:T(8,128)(2,1)S(1)}, u32[]{:S(2)}, u32[]{:S(2)}) collective-permute-start(bf16[4,128,128]{2,1,0:T(8,128)(2,1)S(1)} %get-tuple-element.32), channel_id=1, source_target_pairs={{0,3},{1,4},{2,7},{3,0},{4,1},{5,6},{6,5},{7,2},{8,13},{9,10},{10,... | collective-permute-start | bytes 393224 | tf_op jit(solution)/shard_map/ppermute | solution.py:176
  14.1 0.6 %collective-permute-done.2 = bf16[8,128,128]{2,1,0:T(8,128)(2,1)S(1)} collective-permute-done((bf16[8,128,128]{2,1,0:T(8,128)(2,1)S(1)}, bf16[8,128,128]{2,1,0:T(8,128)(2,1)S(1)}, u32[]{:S(2)}, u32[]{:S(2)}) %collective-permute-start.2) | collective-permute-done | bytes 262176 | tf_op jit(solution)/shard_map/ppermute | solution.py:176
  14.8 1.8 %collective-permute-start.3 = (bf16[4,128,128]{2,1,0:T(8,128)(2,1)S(1)}, bf16[4,128,128]{2,1,0:T(8,128)(2,1)S(1)}, u32[]{:S(2)}, u32[]{:S(2)}) collective-permute-start(bf16[4,128,128]{2,1,0:T(8,128)(2,1)S(1)} %get-tuple-element.34), channel_id=1, source_target_pairs={{0,3},{1,8},{2,11},{3,0},{4,13},{5,6},{6,5},{7,14},{8,1},{9,10},{1... | collective-permute-start | bytes 393224 | tf_op jit(solution)/shard_map/ppermute | solution.py:176
  16.8 2.2 %collective-permute-start.14 = (bf16[2,128,128]{2,1,0:T(8,128)(2,1)S(1)}, bf16[2,128,128]{2,1,0:T(8,128)(2,1)S(1)}, u32[]{:S(2)}, u32[]{:S(2)}) collective-permute-start(bf16[2,128,128]{2,1,0:T(8,128)(2,1)S(1)} %get-tuple-element.36), channel_id=1, source_target_pairs={{0,9},{1,2},{2,1},{3,10},{4,7},{5,12},{6,15},{7,4},{8,11},{9,0},{1... | collective-permute-start | bytes 196616 | tf_op jit(solution)/shard_map/ppermute | solution.py:176
  19.3 1.9 %collective-permute-start.4 = (bf16[2,128,128]{2,1,0:T(8,128)(2,1)S(1)}, bf16[2,128,128]{2,1,0:T(8,128)(2,1)S(1)}, u32[]{:S(2)}, u32[]{:S(2)}) collective-permute-start(bf16[2,128,128]{2,1,0:T(8,128)(2,1)S(1)} %get-tuple-element.38), channel_id=1, source_target_pairs={{0,9},{1,4},{2,7},{3,10},{4,1},{5,12},{6,15},{7,2},{8,13},{9,0},{1... | collective-permute-start | bytes 196616 | tf_op jit(solution)/shard_map/ppermute | solution.py:176
  21.2 2.7 %collective-permute-start.15 = (bf16[1,128,128]{2,1,0:T(8,128)(2,1)S(1)}, bf16[1,128,128]{2,1,0:T(8,128)(2,1)S(1)}, u32[]{:S(2)}, u32[]{:S(2)}) collective-permute-start(bf16[1,128,128]{2,1,0:T(8,128)(2,1)S(1)} %fusion.4), channel_id=1, source_target_pairs={{0,17},{1,16},{2,19},{3,18},{4,21},{5,20},{6,23},{7,22},{8,25},{9,... | collective-permute-start | bytes 98312 | tf_op jit(solution)/shard_map/ppermute | solution.py:176
  23.9 2.1 %collective-permute-start.5 = (bf16[1,128,128]{2,1,0:T(8,128)(2,1)S(1)}, bf16[1,128,128]{2,1,0:T(8,128)(2,1)S(1)}, u32[]{:S(2)}, u32[]{:S(2)}) collective-permute-start(bf16[1,128,128]{2,1,0:T(8,128)(2,1)S(1)} %fusion.6), channel_id=1, source_target_pairs={{0,17},{1,16},{2,19},{3,18},{4,21},{5,20},{6,23},{7,22},{8,25},{9,... | collective-permute-start | bytes 98312 | tf_op jit(solution)/shard_map/ppermute | solution.py:176
  26.1 2.2 %collective-permute-start.16 = (bf16[1,128,128]{2,1,0:T(8,128)(2,1)S(1)}, bf16[1,128,128]{2,1,0:T(8,128)(2,1)S(1)}, u32[]{:S(2)}, u32[]{:S(2)}) collective-permute-start(bf16[1,128,128]{2,1,0:T(8,128)(2,1)S(1)} %get-tuple-element.39), channel_id=1, source_target_pairs={{0,17},{1,16},{2,19},{3,18},{4,21},{5,20},{6,23},{7,22},{8,25},{9,... | collective-permute-start | bytes 98312 | tf_op jit(solution)/shard_map/ppermute | solution.py:176
  28.5 2.0 %collective-permute-start.6 = (bf16[1,128,128]{2,1,0:T(8,128)(2,1)S(1)}, bf16[1,128,128]{2,1,0:T(8,128)(2,1)S(1)}, u32[]{:S(2)}, u32[]{:S(2)}) collective-permute-start(bf16[1,128,128]{2,1,0:T(8,128)(2,1)S(1)} %get-tuple-element.42), channel_id=1, source_target_pairs={{0,17},{1,16},{2,19},{3,18},{4,21},{5,20},{6,23},{7,22},{8,25},{9,... | collective-permute-start | bytes 98312 | tf_op jit(solution)/shard_map/ppermute | solution.py:176
  30.5 0.5 %collective-permute-done.16 = bf16[1,128,128]{2,1,0:T(8,128)(2,1)S(1)} collective-permute-done((bf16[1,128,128]{2,1,0:T(8,128)(2,1)S(1)}, bf16[1,128,128]{2,1,0:T(8,128)(2,1)S(1)}, u32[]{:S(2)}, u32[]{:S(2)}) %collective-permute-start.16) | collective-permute-done | bytes 32800 | tf_op jit(solution)/shard_map/ppermute | solution.py:176
  31.1 1.5 %collective-permute-start.17 = (bf16[2,128,128]{2,1,0:T(8,128)(2,1)S(1)}, bf16[2,128,128]{2,1,0:T(8,128)(2,1)S(1)}, u32[]{:S(2)}, u32[]{:S(2)}) collective-permute-start(bf16[2,128,128]{2,1,0:T(8,128)(2,1)S(1)} %pad_maximum_fusion.6), channel_id=1, source_target_pairs={{0,9},{1,4},{2,7},{3,10},{4,1},{5,12},{6,15},{7,2},{8,13},{9,0},{1... | collective-permute-start | bytes 196616 | tf_op jit(solution)/shard_map/ppermute | solution.py:176
  33.1 1.1 %collective-permute-start.7 = (bf16[2,128,128]{2,1,0:T(8,128)(2,1)S(1)}, bf16[2,128,128]{2,1,0:T(8,128)(2,1)S(1)}, u32[]{:S(2)}, u32[]{:S(2)}) collective-permute-start(bf16[2,128,128]{2,1,0:T(8,128)(2,1)S(1)} %pad_maximum_fusion.5), channel_id=1, source_target_pairs={{0,3},{1,8},{2,11},{3,0},{4,13},{5,6},{6,5},{7,14},{8,1},{9,10},{1... | collective-permute-start | bytes 196616 | tf_op jit(solution)/shard_map/ppermute | solution.py:176
  34.2 0.7 %collective-permute-done.17 = bf16[2,128,128]{2,1,0:T(8,128)(2,1)S(1)} collective-permute-done((bf16[2,128,128]{2,1,0:T(8,128)(2,1)S(1)}, bf16[2,128,128]{2,1,0:T(8,128)(2,1)S(1)}, u32[]{:S(2)}, u32[]{:S(2)}) %collective-permute-start.17) | collective-permute-done | bytes 65568 | tf_op jit(solution)/shard_map/ppermute | solution.py:176
  34.9 2.2 %collective-permute-start.18 = (bf16[4,128,128]{2,1,0:T(8,128)(2,1)S(1)}, bf16[4,128,128]{2,1,0:T(8,128)(2,1)S(1)}, u32[]{:S(2)}, u32[]{:S(2)}) collective-permute-start(bf16[4,128,128]{2,1,0:T(8,128)(2,1)S(1)} %pad_maximum_fusion.4), channel_id=1, source_target_pairs={{0,5},{1,2},{2,1},{3,6},{4,7},{5,0},{6,3},{7,4},{8,11},{9,12},{10,... | collective-permute-start | bytes 393224 | tf_op jit(solution)/shard_map/ppermute | solution.py:176
  37.1 0.9 %collective-permute-start.8 = (bf16[4,128,128]{2,1,0:T(8,128)(2,1)S(1)}, bf16[4,128,128]{2,1,0:T(8,128)(2,1)S(1)}, u32[]{:S(2)}, u32[]{:S(2)}) collective-permute-start(bf16[4,128,128]{2,1,0:T(8,128)(2,1)S(1)} %pad_maximum_fusion.2), channel_id=1, source_target_pairs={{0,9},{1,4},{2,7},{3,10},{4,1},{5,12},{6,15},{7,2},{8,13},{9,0},{1... | collective-permute-start | bytes 393224 | tf_op jit(solution)/shard_map/ppermute | solution.py:176
  38.0 3.5 %collective-permute-done.8 = bf16[4,128,128]{2,1,0:T(8,128)(2,1)S(1)} collective-permute-done((bf16[4,128,128]{2,1,0:T(8,128)(2,1)S(1)}, bf16[4,128,128]{2,1,0:T(8,128)(2,1)S(1)}, u32[]{:S(2)}, u32[]{:S(2)}) %collective-permute-start.8) | collective-permute-done | bytes 131104 | tf_op jit(solution)/shard_map/ppermute | solution.py:176
  41.6 1.6 %collective-permute-start.9 = (bf16[8,128,128]{2,1,0:T(8,128)(2,1)S(1)}, bf16[8,128,128]{2,1,0:T(8,128)(2,1)S(1)}, u32[]{:S(2)}, u32[]{:S(2)}) collective-permute-start(bf16[8,128,128]{2,1,0:T(8,128)(2,1)S(1)} %pad_maximum_fusion.refs_0_), channel_id=1, source_target_pairs={{0,5},{1,2},{2,1},{3,6},{4,7},{5,0},{6,3},{7,4},{8,11},{9,12},{10,... | collective-permute-start | bytes 786440 | tf_op jit(solution)/shard_map/ppermute | solution.py:176
  43.2 1.5 %collective-permute-start.19 = (bf16[8,128,128]{2,1,0:T(8,128)(2,1)S(1)}, bf16[8,128,128]{2,1,0:T(8,128)(2,1)S(1)}, u32[]{:S(2)}, u32[]{:S(2)}) collective-permute-start(bf16[8,128,128]{2,1,0:T(8,128)(2,1)S(1)} %pad_maximum_fusion.1.refs_1_), channel_id=1, source_target_pairs={{0,3},{1,8},{2,11},{3,0},{4,13},{5,6},{6,5},{7,14},{8,1},{9,10},{1... | collective-permute-start | bytes 786440 | tf_op jit(solution)/shard_map/ppermute | solution.py:176
  44.8 0.8 %multiply_subtract_fusion = (f32[256,128]{1,0:T(8,128)}, f32[256,128]{1,0:T(8,128)}, f32[256,128]{1,0:T(8,128)}) fusion(f32[256,128]{1,0:T(8,128)S(1)} %bitcast.117, f32[256,128]{1,0:T(8,128)S(1)} %bitcast.118, f32[128,128]{1,0:T(8,128)S(1)} %get-tuple-element.40, f32[128,128]{1,0:T(8,128)S(1)} %get-tuple-element.41, f32[256,128]{1,0:T(8,128)S(1)} %bitcast.119), kind=kLoop, calls=%fused_computation.21 | loop fusion | flops 491520 | bytes 917504 | tf_op jit(solution)/shard_map/sub | solution.py:29
  45.6 0.5 collective-permute-start.22
  46.1 1.3 %collective-permute-done.9.refs_0_ = bf16[8,128,128]{2,1,0:T(8,128)(2,1)S(1)} collective-permute-done((bf16[8,128,128]{2,1,0:T(8,128)(2,1)S(1)}, bf16[8,128,128]{2,1,0:T(8,128)(2,1)S(1)}, u32[]{:S(2)}, u32[]{:S(2)}) %collective-permute-start.9) | collective-permute-done | bytes 262176 | tf_op jit(solution)/shard_map/ppermute | solution.py:176
  47.4 2.2 %collective-permute-start.21 = (bf16[8,128,128]{2,1,0:T(8,128)(2,1)S(1)}, bf16[8,128,128]{2,1,0:T(8,128)(2,1)S(1)}, u32[]{:S(2)}, u32[]{:S(2)}) collective-permute-start(bf16[8,128,128]{2,1,0:T(8,128)(2,1)S(1)} %collective-permute-done.9.refs_0_), channel_id=1, source_target_pairs={{0,1},{1,0},{2,3},{3,2},{4,5},{5,4},{6,7},{7,6},{8,9},{9,8},{10,11... | collective-permute-start | bytes 786440 | tf_op jit(solution)/shard_map/ppermute | solution.py:172
  49.6 1.1 %collective-permute-done.19.refs_0_ = bf16[8,128,128]{2,1,0:T(8,128)(2,1)S(1)} collective-permute-done((bf16[8,128,128]{2,1,0:T(8,128)(2,1)S(1)}, bf16[8,128,128]{2,1,0:T(8,128)(2,1)S(1)}, u32[]{:S(2)}, u32[]{:S(2)}) %collective-permute-start.19) | collective-permute-done | bytes 262176 | tf_op jit(solution)/shard_map/ppermute | solution.py:176
  50.7 1.2 %scatter_pieces.3.refs_2_ = bf16[8192,128]{1,0:T(8,128)(2,1)} custom-call(bf16[8,128,128]{2,1,0:T(8,128)(2,1)S(1)} %pad_maximum_fusion.refs_0_, bf16[8,128,128]{2,1,0:T(8,128)(2,1)S(1)} %pad_maximum_fusion.1.refs_1_, bf16[8,128,128]{2,1,0:T(8,128)(2,1)S(1)} %collective-permute-done.22.refs_2_, bf16[8,128,128]{2,1,0:T(8,128)(2,1)S(1)} %collective-permute-done.23.refs_3_), custom_call_target="tpu_custom_call" | custom-call | flops 1048576 | bytes 1048576 | tf_op jit(solution)/shard_map/scatter_pieces/pallas_call | solution.py:149
  52.0 0.9 %scatter_pieces.4.refs_2_ = bf16[8192,128]{1,0:T(8,128)(2,1)} custom-call(bf16[8,128,128]{2,1,0:T(8,128)(2,1)S(1)} %collective-permute-done.9.refs_0_, bf16[8,128,128]{2,1,0:T(8,128)(2,1)S(1)} %collective-permute-done.21.refs_1_, bf16[8192,128]{1,0:T(8,128)(2,1)} %scatter_pieces.3.refs_2_), custom_call_target="tpu_custom_call", output_to_operand_aliasing={{}: (2, {})} | custom-call | flops 1048576 | bytes 1048576 | tf_op jit(solution)/shard_map/scatter_pieces/pallas_call | solution.py:149
  52.9 0.9 %scatter_pieces.5 = bf16[8192,128]{1,0:T(8,128)(2,1)} custom-call(bf16[8,128,128]{2,1,0:T(8,128)(2,1)S(1)} %collective-permute-done.19.refs_0_, bf16[8,128,128]{2,1,0:T(8,128)(2,1)S(1)} %collective-permute-done.20.refs_1_, bf16[8192,128]{1,0:T(8,128)(2,1)} %scatter_pieces.4.refs_2_), custom_call_target="tpu_custom_call", output_to_operand_aliasing={{}: (2, {})} | custom-call | flops 1048576 | bytes 1048576 | tf_op jit(solution)/shard_map/scatter_pieces/pallas_call | solution.py:149
  (56 shorter events, 2.9 us)
Async XLA Ops:
  0.6 4.2 %copy-start.1 = (f32[2,16384]{1,0:T(2,128)S(1)}, f32[2,16384]{1,0:T(2,128)}, u32[]{:S(2)}) copy-start(f32[2,16384]{1,0:T(2,128)} %param.6) | copy-start | bytes 393220
  0.6 4.2 %copy-start.2 = (f32[2,16384]{1,0:T(2,128)S(1)}, f32[2,16384]{1,0:T(2,128)}, u32[]{:S(2)}) copy-start(f32[2,16384]{1,0:T(2,128)} %param.7) | copy-start | bytes 393220
  0.7 4.4 %copy-start = (f32[2,16384]{1,0:T(2,128)S(1)}, f32[2,16384]{1,0:T(2,128)}, u32[]{:S(2)}) copy-start(f32[2,16384]{1,0:T(2,128)} %param.5) | copy-start | bytes 393220
  2.2 2.8 %collective-permute-start.11 = (bf16[8,128,128]{2,1,0:T(8,128)(2,1)S(1)}, bf16[8,128,128]{2,1,0:T(8,128)(2,1)S(1)}, u32[]{:S(2)}, u32[]{:S(2)}) collective-permute-start(bf16[8,128,128]{2,1,0:T(8,128)(2,1)S(1)} %get-tuple-element.23), channel_id=1, source_target_pairs={{0,1},{1,0},{2,3},{3,2},{4,5},{5,4},{6,7},{7,6},{8,9},{9,8},{10,11... | collective-permute-start | bytes 786440 | tf_op jit(solution)/shard_map/ppermute | solution.py:172
  4.2 5.1 %collective-permute-start.10 = (bf16[8,128,128]{2,1,0:T(8,128)(2,1)S(1)}, bf16[8,128,128]{2,1,0:T(8,128)(2,1)S(1)}, u32[]{:S(2)}, u32[]{:S(2)}) collective-permute-start(bf16[8,128,128]{2,1,0:T(8,128)(2,1)S(1)} %get-tuple-element.21), channel_id=1, source_target_pairs={{0,1},{1,0},{2,3},{3,2},{4,5},{5,4},{6,7},{7,6},{8,9},{9,8},{10,11... | collective-permute-start | bytes 786440 | tf_op jit(solution)/shard_map/ppermute | solution.py:172
  4.3 5.0 %collective-permute-start = (bf16[8,128,128]{2,1,0:T(8,128)(2,1)S(1)}, bf16[8,128,128]{2,1,0:T(8,128)(2,1)S(1)}, u32[]{:S(2)}, u32[]{:S(2)}) collective-permute-start(bf16[8,128,128]{2,1,0:T(8,128)(2,1)S(1)} %get-tuple-element.17), channel_id=1, source_target_pairs={{0,1},{1,0},{2,3},{3,2},{4,5},{5,4},{6,7},{7,6},{8,9},{9,8},{10,11... | collective-permute-start | bytes 786440 | tf_op jit(solution)/shard_map/ppermute | solution.py:172
  4.8 3.0 %collective-permute-start.1 = (bf16[8,128,128]{2,1,0:T(8,128)(2,1)S(1)}, bf16[8,128,128]{2,1,0:T(8,128)(2,1)S(1)}, u32[]{:S(2)}, u32[]{:S(2)}) collective-permute-start(bf16[8,128,128]{2,1,0:T(8,128)(2,1)S(1)} %get-tuple-element.19), channel_id=1, source_target_pairs={{0,1},{1,0},{2,3},{3,2},{4,5},{5,4},{6,7},{7,6},{8,9},{9,8},{10,11... | collective-permute-start | bytes 786440 | tf_op jit(solution)/shard_map/ppermute | solution.py:172
  5.1 6.7 %collective-permute-start.12 = (bf16[8,128,128]{2,1,0:T(8,128)(2,1)S(1)}, bf16[8,128,128]{2,1,0:T(8,128)(2,1)S(1)}, u32[]{:S(2)}, u32[]{:S(2)}) collective-permute-start(bf16[8,128,128]{2,1,0:T(8,128)(2,1)S(1)} %add_convert_fusion), channel_id=1, source_target_pairs={{0,5},{1,8},{2,11},{3,6},{4,13},{5,0},{6,3},{7,14},{8,1},{9,12},{1... | collective-permute-start | bytes 786440 | tf_op jit(solution)/shard_map/ppermute | solution.py:176
  7.9 6.8 %collective-permute-start.2 = (bf16[8,128,128]{2,1,0:T(8,128)(2,1)S(1)}, bf16[8,128,128]{2,1,0:T(8,128)(2,1)S(1)}, u32[]{:S(2)}, u32[]{:S(2)}) collective-permute-start(bf16[8,128,128]{2,1,0:T(8,128)(2,1)S(1)} %add_convert_fusion.1), channel_id=1, source_target_pairs={{0,5},{1,2},{2,1},{3,6},{4,7},{5,0},{6,3},{7,4},{8,11},{9,12},{10,... | collective-permute-start | bytes 786440 | tf_op jit(solution)/shard_map/ppermute | solution.py:176
  11.9 4.8 %collective-permute-start.13 = (bf16[4,128,128]{2,1,0:T(8,128)(2,1)S(1)}, bf16[4,128,128]{2,1,0:T(8,128)(2,1)S(1)}, u32[]{:S(2)}, u32[]{:S(2)}) collective-permute-start(bf16[4,128,128]{2,1,0:T(8,128)(2,1)S(1)} %get-tuple-element.32), channel_id=1, source_target_pairs={{0,3},{1,4},{2,7},{3,0},{4,1},{5,6},{6,5},{7,2},{8,13},{9,10},{10,... | collective-permute-start | bytes 393224 | tf_op jit(solution)/shard_map/ppermute | solution.py:176
  14.8 4.5 %collective-permute-start.3 = (bf16[4,128,128]{2,1,0:T(8,128)(2,1)S(1)}, bf16[4,128,128]{2,1,0:T(8,128)(2,1)S(1)}, u32[]{:S(2)}, u32[]{:S(2)}) collective-permute-start(bf16[4,128,128]{2,1,0:T(8,128)(2,1)S(1)} %get-tuple-element.34), channel_id=1, source_target_pairs={{0,3},{1,8},{2,11},{3,0},{4,13},{5,6},{6,5},{7,14},{8,1},{9,10},{1... | collective-permute-start | bytes 393224 | tf_op jit(solution)/shard_map/ppermute | solution.py:176
  16.8 4.4 %collective-permute-start.14 = (bf16[2,128,128]{2,1,0:T(8,128)(2,1)S(1)}, bf16[2,128,128]{2,1,0:T(8,128)(2,1)S(1)}, u32[]{:S(2)}, u32[]{:S(2)}) collective-permute-start(bf16[2,128,128]{2,1,0:T(8,128)(2,1)S(1)} %get-tuple-element.36), channel_id=1, source_target_pairs={{0,9},{1,2},{2,1},{3,10},{4,7},{5,12},{6,15},{7,4},{8,11},{9,0},{1... | collective-permute-start | bytes 196616 | tf_op jit(solution)/shard_map/ppermute | solution.py:176
  19.3 4.6 %collective-permute-start.4 = (bf16[2,128,128]{2,1,0:T(8,128)(2,1)S(1)}, bf16[2,128,128]{2,1,0:T(8,128)(2,1)S(1)}, u32[]{:S(2)}, u32[]{:S(2)}) collective-permute-start(bf16[2,128,128]{2,1,0:T(8,128)(2,1)S(1)} %get-tuple-element.38), channel_id=1, source_target_pairs={{0,9},{1,4},{2,7},{3,10},{4,1},{5,12},{6,15},{7,2},{8,13},{9,0},{1... | collective-permute-start | bytes 196616 | tf_op jit(solution)/shard_map/ppermute | solution.py:176
  21.2 4.9 %collective-permute-start.15 = (bf16[1,128,128]{2,1,0:T(8,128)(2,1)S(1)}, bf16[1,128,128]{2,1,0:T(8,128)(2,1)S(1)}, u32[]{:S(2)}, u32[]{:S(2)}) collective-permute-start(bf16[1,128,128]{2,1,0:T(8,128)(2,1)S(1)} %fusion.4), channel_id=1, source_target_pairs={{0,17},{1,16},{2,19},{3,18},{4,21},{5,20},{6,23},{7,22},{8,25},{9,... | collective-permute-start | bytes 98312 | tf_op jit(solution)/shard_map/ppermute | solution.py:176
  23.9 4.5 %collective-permute-start.5 = (bf16[1,128,128]{2,1,0:T(8,128)(2,1)S(1)}, bf16[1,128,128]{2,1,0:T(8,128)(2,1)S(1)}, u32[]{:S(2)}, u32[]{:S(2)}) collective-permute-start(bf16[1,128,128]{2,1,0:T(8,128)(2,1)S(1)} %fusion.6), channel_id=1, source_target_pairs={{0,17},{1,16},{2,19},{3,18},{4,21},{5,20},{6,23},{7,22},{8,25},{9,... | collective-permute-start | bytes 98312 | tf_op jit(solution)/shard_map/ppermute | solution.py:176
  26.1 5.0 %collective-permute-start.16 = (bf16[1,128,128]{2,1,0:T(8,128)(2,1)S(1)}, bf16[1,128,128]{2,1,0:T(8,128)(2,1)S(1)}, u32[]{:S(2)}, u32[]{:S(2)}) collective-permute-start(bf16[1,128,128]{2,1,0:T(8,128)(2,1)S(1)} %get-tuple-element.39), channel_id=1, source_target_pairs={{0,17},{1,16},{2,19},{3,18},{4,21},{5,20},{6,23},{7,22},{8,25},{9,... | collective-permute-start | bytes 98312 | tf_op jit(solution)/shard_map/ppermute | solution.py:176
  28.5 4.5 %collective-permute-start.6 = (bf16[1,128,128]{2,1,0:T(8,128)(2,1)S(1)}, bf16[1,128,128]{2,1,0:T(8,128)(2,1)S(1)}, u32[]{:S(2)}, u32[]{:S(2)}) collective-permute-start(bf16[1,128,128]{2,1,0:T(8,128)(2,1)S(1)} %get-tuple-element.42), channel_id=1, source_target_pairs={{0,17},{1,16},{2,19},{3,18},{4,21},{5,20},{6,23},{7,22},{8,25},{9,... | collective-permute-start | bytes 98312 | tf_op jit(solution)/shard_map/ppermute | solution.py:176
  31.1 3.8 %collective-permute-start.17 = (bf16[2,128,128]{2,1,0:T(8,128)(2,1)S(1)}, bf16[2,128,128]{2,1,0:T(8,128)(2,1)S(1)}, u32[]{:S(2)}, u32[]{:S(2)}) collective-permute-start(bf16[2,128,128]{2,1,0:T(8,128)(2,1)S(1)} %pad_maximum_fusion.6), channel_id=1, source_target_pairs={{0,9},{1,4},{2,7},{3,10},{4,1},{5,12},{6,15},{7,2},{8,13},{9,0},{1... | collective-permute-start | bytes 196616 | tf_op jit(solution)/shard_map/ppermute | solution.py:176
  33.1 4.0 %collective-permute-start.7 = (bf16[2,128,128]{2,1,0:T(8,128)(2,1)S(1)}, bf16[2,128,128]{2,1,0:T(8,128)(2,1)S(1)}, u32[]{:S(2)}, u32[]{:S(2)}) collective-permute-start(bf16[2,128,128]{2,1,0:T(8,128)(2,1)S(1)} %pad_maximum_fusion.5), channel_id=1, source_target_pairs={{0,3},{1,8},{2,11},{3,0},{4,13},{5,6},{6,5},{7,14},{8,1},{9,10},{1... | collective-permute-start | bytes 196616 | tf_op jit(solution)/shard_map/ppermute | solution.py:176
  34.9 8.3 %collective-permute-start.18 = (bf16[4,128,128]{2,1,0:T(8,128)(2,1)S(1)}, bf16[4,128,128]{2,1,0:T(8,128)(2,1)S(1)}, u32[]{:S(2)}, u32[]{:S(2)}) collective-permute-start(bf16[4,128,128]{2,1,0:T(8,128)(2,1)S(1)} %pad_maximum_fusion.4), channel_id=1, source_target_pairs={{0,5},{1,2},{2,1},{3,6},{4,7},{5,0},{6,3},{7,4},{8,11},{9,12},{10,... | collective-permute-start | bytes 393224 | tf_op jit(solution)/shard_map/ppermute | solution.py:176
  37.1 4.5 %collective-permute-start.8 = (bf16[4,128,128]{2,1,0:T(8,128)(2,1)S(1)}, bf16[4,128,128]{2,1,0:T(8,128)(2,1)S(1)}, u32[]{:S(2)}, u32[]{:S(2)}) collective-permute-start(bf16[4,128,128]{2,1,0:T(8,128)(2,1)S(1)} %pad_maximum_fusion.2), channel_id=1, source_target_pairs={{0,9},{1,4},{2,7},{3,10},{4,1},{5,12},{6,15},{7,2},{8,13},{9,0},{1... | collective-permute-start | bytes 393224 | tf_op jit(solution)/shard_map/ppermute | solution.py:176
  41.6 5.9 %collective-permute-start.9 = (bf16[8,128,128]{2,1,0:T(8,128)(2,1)S(1)}, bf16[8,128,128]{2,1,0:T(8,128)(2,1)S(1)}, u32[]{:S(2)}, u32[]{:S(2)}) collective-permute-start(bf16[8,128,128]{2,1,0:T(8,128)(2,1)S(1)} %pad_maximum_fusion.refs_0_), channel_id=1, source_target_pairs={{0,5},{1,2},{2,1},{3,6},{4,7},{5,0},{6,3},{7,4},{8,11},{9,12},{10,... | collective-permute-start | bytes 786440 | tf_op jit(solution)/shard_map/ppermute | solution.py:176
  43.2 7.5 %collective-permute-start.19 = (bf16[8,128,128]{2,1,0:T(8,128)(2,1)S(1)}, bf16[8,128,128]{2,1,0:T(8,128)(2,1)S(1)}, u32[]{:S(2)}, u32[]{:S(2)}) collective-permute-start(bf16[8,128,128]{2,1,0:T(8,128)(2,1)S(1)} %pad_maximum_fusion.1.refs_1_), channel_id=1, source_target_pairs={{0,3},{1,8},{2,11},{3,0},{4,13},{5,6},{6,5},{7,14},{8,1},{9,10},{1... | collective-permute-start | bytes 786440 | tf_op jit(solution)/shard_map/ppermute | solution.py:176
  45.6 5.1 %collective-permute-start.23 = (bf16[8,128,128]{2,1,0:T(8,128)(2,1)S(1)}, bf16[8,128,128]{2,1,0:T(8,128)(2,1)S(1)}, u32[]{:S(2)}, u32[]{:S(2)}) collective-permute-start(bf16[8,128,128]{2,1,0:T(8,128)(2,1)S(1)} %pad_maximum_fusion.1.refs_1_), channel_id=1, source_target_pairs={{0,1},{1,0},{2,3},{3,2},{4,5},{5,4},{6,7},{7,6},{8,9},{9,8},{10,11... | collective-permute-start | bytes 786440 | tf_op jit(solution)/shard_map/ppermute | solution.py:172
  45.6 5.1 %collective-permute-start.22 = (bf16[8,128,128]{2,1,0:T(8,128)(2,1)S(1)}, bf16[8,128,128]{2,1,0:T(8,128)(2,1)S(1)}, u32[]{:S(2)}, u32[]{:S(2)}) collective-permute-start(bf16[8,128,128]{2,1,0:T(8,128)(2,1)S(1)} %pad_maximum_fusion.refs_0_), channel_id=1, source_target_pairs={{0,1},{1,0},{2,3},{3,2},{4,5},{5,4},{6,7},{7,6},{8,9},{9,8},{10,11... | collective-permute-start | bytes 786440 | tf_op jit(solution)/shard_map/ppermute | solution.py:172
  47.4 4.5 %collective-permute-start.21 = (bf16[8,128,128]{2,1,0:T(8,128)(2,1)S(1)}, bf16[8,128,128]{2,1,0:T(8,128)(2,1)S(1)}, u32[]{:S(2)}, u32[]{:S(2)}) collective-permute-start(bf16[8,128,128]{2,1,0:T(8,128)(2,1)S(1)} %collective-permute-done.9.refs_0_), channel_id=1, source_target_pairs={{0,1},{1,0},{2,3},{3,2},{4,5},{5,4},{6,7},{7,6},{8,9},{9,8},{10,11... | collective-permute-start | bytes 786440 | tf_op jit(solution)/shard_map/ppermute | solution.py:172
  50.7 2.2 %collective-permute-start.20 = (bf16[8,128,128]{2,1,0:T(8,128)(2,1)S(1)}, bf16[8,128,128]{2,1,0:T(8,128)(2,1)S(1)}, u32[]{:S(2)}, u32[]{:S(2)}) collective-permute-start(bf16[8,128,128]{2,1,0:T(8,128)(2,1)S(1)} %collective-permute-done.19.refs_0_), channel_id=1, source_target_pairs={{0,1},{1,0},{2,3},{3,2},{4,5},{5,4},{6,7},{7,6},{8,9},{9,8},{10,11... | collective-permute-start | bytes 786440 | tf_op jit(solution)/shard_map/ppermute | solution.py:172
where the time goes:
time: 54.1 us; the launch traced here: 53.9 us
  starting transfers between devices  33.8 us (62%)
  waiting for transfers between devices  11.2 us (21%)
  Pallas kernels  6.09 us (11%)
  other arithmetic  1.91 us (4%)
  between operations  0.89 us (2%)
    ppermute x16, starting transfers between devices, swap_chips(): lax.ppermute(x, AXES, [(i, i ^ part.mask(team[i], step)) for i in range(d...  29.9 us
    ppermute x16, waiting for transfers between devices, swap_chips(): lax.ppermute(x, AXES, [(i, i ^ part.mask(team[i], step)) for i in range(d...  11.1 us
    ppermute x8, starting transfers between devices, swap_cores(): return lax.ppermute(x, AXES, [(i, i ^ 1) for i in range(devices)])  3.92 us
    pallas_call x3, Pallas kernels, scatter_pieces(): pl.pallas_call(body, out_shape=jax.ShapeDtypeStruct((total, LANES), block...  3.12 us
    pallas_call x2, Pallas kernels, gather_pieces(): pl.pallas_call(body, out_shape=outs, in_specs=[pl.BlockSpec(memory_space=...  2.97 us
  transfers between devices with their start and end apart: 24, of which 11 were waited for; matrix products, arithmetic and copies ran while one was open for 4% of the time, Pallas kernels for 7%

commit v1 on v0

--- a/solution.py
+++ b/solution.py
@@ -18,7 +18,7 @@
 SHARES = (0, 8)
 GATHER_GRANT = 52 << 20
 SUM_ORDERS = (((X, Y, Z), (Y, Z, X)), ((X, Y, Z), (Z, X, Y)))
-SPREAD_ORDERS = (((X, Z, Y), (Y, X, Z)), ((Y, X, Z), (Z, Y, X)))
+SPREAD_ORDERS = (((Z, Y, X), (X, Z, Y)), ((Z, Y, X), (Y, Z, X)))
 
 
 def adam_update(mean_grad, master_params, first_moment, second_moment):
@@ -213,7 +213,8 @@
     outs = adam_update(jnp.concatenate(sums, axis=0) / devices, *state)
     total = devices * rows
     early = [(p, True, 0, x) for p, x in zip(routes, held)]
-    early += [(p, False, 0, swap_cores(x)) for p, x in zip(routes, held)]
+    for n, part in enumerate(routes):
+        early.append((part, False, 0, swap_cores(held[n])))
     new_weights = scatter_pieces(None, early, rows, total)
     for n, part in enumerate(routes):
         high = swap_chips(held[n], part, 0)

time: 54.1 us -> 53.6 us (level)
  starting transfers between devices: 33.8 us -> 31.9 us
  waiting for transfers between devices: 11.2 us -> 12.5 us
    ppermute x16, waiting for transfers between devices: 11.1 us -> 12.5 us  [swap_chips(): lax.ppermute(x, AXES, [(i, i ^ part.mask(team[i], step)) for i in range(d...]
    ppermute x16, starting transfers between devices: 29.9 us -> 28.9 us  [swap_chips(): lax.ppermute(x, AXES, [(i, i ^ part.mask(team[i], step)) for i in range(d...]
    ppermute x8, starting transfers between devices: 3.92 us -> 3.02 us  [swap_cores(): return lax.ppermute(x, AXES, [(i, i ^ 1) for i in range(devices)])]
where the time goes in v1:
time: 53.6 us; the launch traced here: 53.3 us
  starting transfers between devices  31.9 us (60%)
  waiting for transfers between devices  12.5 us (23%)
  Pallas kernels  6.09 us (11%)
  other arithmetic  1.91 us (4%)
  between operations  0.89 us (2%)
    ppermute x16, starting transfers between devices, swap_chips(): lax.ppermute(x, AXES, [(i, i ^ part.mask(team[i], step)) for i in range(d...  28.9 us
    ppermute x16, waiting for transfers between devices, swap_chips(): lax.ppermute(x, AXES, [(i, i ^ part.mask(team[i], step)) for i in range(d...  12.5 us
    pallas_call x3, Pallas kernels, scatter_pieces(): pl.pallas_call(body, out_shape=jax.ShapeDtypeStruct((total, LANES), block...  3.11 us
    ppermute x8, starting transfers between devices, swap_cores(): return lax.ppermute(x, AXES, [(i, i ^ 1) for i in range(devices)])  3.02 us
    pallas_call x2, Pallas kernels, gather_pieces(): pl.pallas_call(body, out_shape=outs, in_specs=[pl.BlockSpec(memory_space=...  2.97 us
  transfers between devices with their start and end apart: 24, of which 11 were waited for; matrix products, arithmetic and copies ran while one was open for 4% of the time, Pallas kernels for 7%

profile of v1, /device:TPU:0, one launch (start us, length us, event | category | flops | bytes accessed | tf_op | source)
XLA Modules:
  0.0 53.3 jit_solution(7182313042321300489)
XLA Ops:
  0.7 1.5 %gather_pieces.3 = (bf16[8,128,128]{2,1,0:T(8,128)(2,1)S(1)}, bf16[8,128,128]{2,1,0:T(8,128)(2,1)S(1)}, bf16[8,128,128]{2,1,0:T(8,128)(2,1)S(1)}, bf16[8,128,128]{2,1,0:T(8,128)(2,1)S(1)}) custom-call(bf16[8192,128]{1,0:T(8,128)(2,1)} %bitcast.114), custom_call_target="tpu_custom_call" | custom-call | flops 1048576 | bytes 1048576 | tf_op jit(solution)/shard_map/gather_pieces/pallas_call | solution.py:119
  2.2 0.6 %collective-permute-start.11 = (bf16[8,128,128]{2,1,0:T(8,128)(2,1)S(1)}, bf16[8,128,128]{2,1,0:T(8,128)(2,1)S(1)}, u32[]{:S(2)}, u32[]{:S(2)}) collective-permute-start(bf16[8,128,128]{2,1,0:T(8,128)(2,1)S(1)} %get-tuple-element.23), channel_id=1, source_target_pairs={{0,1},{1,0},{2,3},{3,2},{4,5},{5,4},{6,7},{7,6},{8,9},{9,8},{10,11... | collective-permute-start | bytes 786440 | tf_op jit(solution)/shard_map/ppermute | solution.py:172
  2.8 1.4 %gather_pieces.2 = (bf16[8,128,128]{2,1,0:T(8,128)(2,1)S(1)}, bf16[8,128,128]{2,1,0:T(8,128)(2,1)S(1)}, bf16[8,128,128]{2,1,0:T(8,128)(2,1)S(1)}, bf16[8,128,128]{2,1,0:T(8,128)(2,1)S(1)}) custom-call(bf16[8192,128]{1,0:T(8,128)(2,1)} %bitcast.115), custom_call_target="tpu_custom_call" | custom-call | flops 1048576 | bytes 1048576 | tf_op jit(solution)/shard_map/gather_pieces/pallas_call | solution.py:119
  4.3 0.5 collective-permute-start
  5.1 2.7 %collective-permute-start.12 = (bf16[8,128,128]{2,1,0:T(8,128)(2,1)S(1)}, bf16[8,128,128]{2,1,0:T(8,128)(2,1)S(1)}, u32[]{:S(2)}, u32[]{:S(2)}) collective-permute-start(bf16[8,128,128]{2,1,0:T(8,128)(2,1)S(1)} %add_convert_fusion), channel_id=1, source_target_pairs={{0,5},{1,8},{2,11},{3,6},{4,13},{5,0},{6,3},{7,14},{8,1},{9,12},{1... | collective-permute-start | bytes 786440 | tf_op jit(solution)/shard_map/ppermute | solution.py:176
  7.9 1.4 %collective-permute-start.2 = (bf16[8,128,128]{2,1,0:T(8,128)(2,1)S(1)}, bf16[8,128,128]{2,1,0:T(8,128)(2,1)S(1)}, u32[]{:S(2)}, u32[]{:S(2)}) collective-permute-start(bf16[8,128,128]{2,1,0:T(8,128)(2,1)S(1)} %add_convert_fusion.1), channel_id=1, source_target_pairs={{0,5},{1,2},{2,1},{3,6},{4,7},{5,0},{6,3},{7,4},{8,11},{9,12},{10,... | collective-permute-start | bytes 786440 | tf_op jit(solution)/shard_map/ppermute | solution.py:176
  9.4 2.4 %collective-permute-done.12 = bf16[8,128,128]{2,1,0:T(8,128)(2,1)S(1)} collective-permute-done((bf16[8,128,128]{2,1,0:T(8,128)(2,1)S(1)}, bf16[8,128,128]{2,1,0:T(8,128)(2,1)S(1)}, u32[]{:S(2)}, u32[]{:S(2)}) %collective-permute-start.12) | collective-permute-done | bytes 262176 | tf_op jit(solution)/shard_map/ppermute | solution.py:176
  11.9 2.1 %collective-permute-start.13 = (bf16[4,128,128]{2,1,0:T(8,128)(2,1)S(1)}, bf16[4,128,128]{2,1,0:T(8,128)(2,1)S(1)}, u32[]{:S(2)}, u32[]{:S(2)}) collective-permute-start(bf16[4,128,128]{2,1,0:T(8,128)(2,1)S(1)} %get-tuple-element.32), channel_id=1, source_target_pairs={{0,3},{1,4},{2,7},{3,0},{4,1},{5,6},{6,5},{7,2},{8,13},{9,10},{10,... | collective-permute-start | bytes 393224 | tf_op jit(solution)/shard_map/ppermute | solution.py:176
  14.1 0.6 %collective-permute-done.2 = bf16[8,128,128]{2,1,0:T(8,128)(2,1)S(1)} collective-permute-done((bf16[8,128,128]{2,1,0:T(8,128)(2,1)S(1)}, bf16[8,128,128]{2,1,0:T(8,128)(2,1)S(1)}, u32[]{:S(2)}, u32[]{:S(2)}) %collective-permute-start.2) | collective-permute-done | bytes 262176 | tf_op jit(solution)/shard_map/ppermute | solution.py:176
  14.8 1.8 %collective-permute-start.3 = (bf16[4,128,128]{2,1,0:T(8,128)(2,1)S(1)}, bf16[4,128,128]{2,1,0:T(8,128)(2,1)S(1)}, u32[]{:S(2)}, u32[]{:S(2)}) collective-permute-start(bf16[4,128,128]{2,1,0:T(8,128)(2,1)S(1)} %get-tuple-element.34), channel_id=1, source_target_pairs={{0,3},{1,8},{2,11},{3,0},{4,13},{5,6},{6,5},{7,14},{8,1},{9,10},{1... | collective-permute-start | bytes 393224 | tf_op jit(solution)/shard_map/ppermute | solution.py:176
  16.8 2.2 %collective-permute-start.14 = (bf16[2,128,128]{2,1,0:T(8,128)(2,1)S(1)}, bf16[2,128,128]{2,1,0:T(8,128)(2,1)S(1)}, u32[]{:S(2)}, u32[]{:S(2)}) collective-permute-start(bf16[2,128,128]{2,1,0:T(8,128)(2,1)S(1)} %get-tuple-element.36), channel_id=1, source_target_pairs={{0,9},{1,2},{2,1},{3,10},{4,7},{5,12},{6,15},{7,4},{8,11},{9,0},{1... | collective-permute-start | bytes 196616 | tf_op jit(solution)/shard_map/ppermute | solution.py:176
  19.3 1.9 %collective-permute-start.4 = (bf16[2,128,128]{2,1,0:T(8,128)(2,1)S(1)}, bf16[2,128,128]{2,1,0:T(8,128)(2,1)S(1)}, u32[]{:S(2)}, u32[]{:S(2)}) collective-permute-start(bf16[2,128,128]{2,1,0:T(8,128)(2,1)S(1)} %get-tuple-element.38), channel_id=1, source_target_pairs={{0,9},{1,4},{2,7},{3,10},{4,1},{5,12},{6,15},{7,2},{8,13},{9,0},{1... | collective-permute-start | bytes 196616 | tf_op jit(solution)/shard_map/ppermute | solution.py:176
  21.2 2.7 %collective-permute-start.15 = (bf16[1,128,128]{2,1,0:T(8,128)(2,1)S(1)}, bf16[1,128,128]{2,1,0:T(8,128)(2,1)S(1)}, u32[]{:S(2)}, u32[]{:S(2)}) collective-permute-start(bf16[1,128,128]{2,1,0:T(8,128)(2,1)S(1)} %fusion.4), channel_id=1, source_target_pairs={{0,17},{1,16},{2,19},{3,18},{4,21},{5,20},{6,23},{7,22},{8,25},{9,... | collective-permute-start | bytes 98312 | tf_op jit(solution)/shard_map/ppermute | solution.py:176
  23.9 2.1 %collective-permute-start.5 = (bf16[1,128,128]{2,1,0:T(8,128)(2,1)S(1)}, bf16[1,128,128]{2,1,0:T(8,128)(2,1)S(1)}, u32[]{:S(2)}, u32[]{:S(2)}) collective-permute-start(bf16[1,128,128]{2,1,0:T(8,128)(2,1)S(1)} %fusion.6), channel_id=1, source_target_pairs={{0,17},{1,16},{2,19},{3,18},{4,21},{5,20},{6,23},{7,22},{8,25},{9,... | collective-permute-start | bytes 98312 | tf_op jit(solution)/shard_map/ppermute | solution.py:176
  26.1 2.2 %collective-permute-start.16 = (bf16[1,128,128]{2,1,0:T(8,128)(2,1)S(1)}, bf16[1,128,128]{2,1,0:T(8,128)(2,1)S(1)}, u32[]{:S(2)}, u32[]{:S(2)}) collective-permute-start(bf16[1,128,128]{2,1,0:T(8,128)(2,1)S(1)} %get-tuple-element.39), channel_id=1, source_target_pairs={{0,17},{1,16},{2,19},{3,18},{4,21},{5,20},{6,23},{7,22},{8,25},{9,... | collective-permute-start | bytes 98312 | tf_op jit(solution)/shard_map/ppermute | solution.py:176
  28.5 2.0 %collective-permute-start.6 = (bf16[1,128,128]{2,1,0:T(8,128)(2,1)S(1)}, bf16[1,128,128]{2,1,0:T(8,128)(2,1)S(1)}, u32[]{:S(2)}, u32[]{:S(2)}) collective-permute-start(bf16[1,128,128]{2,1,0:T(8,128)(2,1)S(1)} %get-tuple-element.42), channel_id=1, source_target_pairs={{0,17},{1,16},{2,19},{3,18},{4,21},{5,20},{6,23},{7,22},{8,25},{9,... | collective-permute-start | bytes 98312 | tf_op jit(solution)/shard_map/ppermute | solution.py:176
  30.5 0.5 %collective-permute-done.16 = bf16[1,128,128]{2,1,0:T(8,128)(2,1)S(1)} collective-permute-done((bf16[1,128,128]{2,1,0:T(8,128)(2,1)S(1)}, bf16[1,128,128]{2,1,0:T(8,128)(2,1)S(1)}, u32[]{:S(2)}, u32[]{:S(2)}) %collective-permute-start.16) | collective-permute-done | bytes 32800 | tf_op jit(solution)/shard_map/ppermute | solution.py:176
  31.1 1.8 %collective-permute-start.17 = (bf16[2,128,128]{2,1,0:T(8,128)(2,1)S(1)}, bf16[2,128,128]{2,1,0:T(8,128)(2,1)S(1)}, u32[]{:S(2)}, u32[]{:S(2)}) collective-permute-start(bf16[2,128,128]{2,1,0:T(8,128)(2,1)S(1)} %pad_maximum_fusion.6), channel_id=1, source_target_pairs={{0,5},{1,4},{2,7},{3,6},{4,1},{5,0},{6,3},{7,2},{8,13},{9,12},{10,... | collective-permute-start | bytes 196616 | tf_op jit(solution)/shard_map/ppermute | solution.py:176
  33.1 1.1 %collective-permute-start.7 = (bf16[2,128,128]{2,1,0:T(8,128)(2,1)S(1)}, bf16[2,128,128]{2,1,0:T(8,128)(2,1)S(1)}, u32[]{:S(2)}, u32[]{:S(2)}) collective-permute-start(bf16[2,128,128]{2,1,0:T(8,128)(2,1)S(1)} %pad_maximum_fusion.5), channel_id=1, source_target_pairs={{0,5},{1,2},{2,1},{3,6},{4,7},{5,0},{6,3},{7,4},{8,11},{9,12},{10,... | collective-permute-start | bytes 196616 | tf_op jit(solution)/shard_map/ppermute | solution.py:176
  34.2 1.1 %collective-permute-done.17 = bf16[2,128,128]{2,1,0:T(8,128)(2,1)S(1)} collective-permute-done((bf16[2,128,128]{2,1,0:T(8,128)(2,1)S(1)}, bf16[2,128,128]{2,1,0:T(8,128)(2,1)S(1)}, u32[]{:S(2)}, u32[]{:S(2)}) %collective-permute-start.17) | collective-permute-done | bytes 65568 | tf_op jit(solution)/shard_map/ppermute | solution.py:176
  35.3 1.7 %collective-permute-start.18 = (bf16[4,128,128]{2,1,0:T(8,128)(2,1)S(1)}, bf16[4,128,128]{2,1,0:T(8,128)(2,1)S(1)}, u32[]{:S(2)}, u32[]{:S(2)}) collective-permute-start(bf16[4,128,128]{2,1,0:T(8,128)(2,1)S(1)} %pad_maximum_fusion.4), channel_id=1, source_target_pairs={{0,3},{1,8},{2,11},{3,0},{4,13},{5,6},{6,5},{7,14},{8,1},{9,10},{1... | collective-permute-start | bytes 393224 | tf_op jit(solution)/shard_map/ppermute | solution.py:176
  37.0 1.4 %collective-permute-start.8 = (bf16[4,128,128]{2,1,0:T(8,128)(2,1)S(1)}, bf16[4,128,128]{2,1,0:T(8,128)(2,1)S(1)}, u32[]{:S(2)}, u32[]{:S(2)}) collective-permute-start(bf16[4,128,128]{2,1,0:T(8,128)(2,1)S(1)} %pad_maximum_fusion.2), channel_id=1, source_target_pairs={{0,3},{1,8},{2,11},{3,0},{4,13},{5,6},{6,5},{7,14},{8,1},{9,10},{1... | collective-permute-start | bytes 393224 | tf_op jit(solution)/shard_map/ppermute | solution.py:176
  38.5 3.0 %collective-permute-done.8 = bf16[4,128,128]{2,1,0:T(8,128)(2,1)S(1)} collective-permute-done((bf16[4,128,128]{2,1,0:T(8,128)(2,1)S(1)}, bf16[4,128,128]{2,1,0:T(8,128)(2,1)S(1)}, u32[]{:S(2)}, u32[]{:S(2)}) %collective-permute-start.8) | collective-permute-done | bytes 131104 | tf_op jit(solution)/shard_map/ppermute | solution.py:176
  41.5 1.0 %collective-permute-start.9 = (bf16[8,128,128]{2,1,0:T(8,128)(2,1)S(1)}, bf16[8,128,128]{2,1,0:T(8,128)(2,1)S(1)}, u32[]{:S(2)}, u32[]{:S(2)}) collective-permute-start(bf16[8,128,128]{2,1,0:T(8,128)(2,1)S(1)} %pad_maximum_fusion.refs_0_), channel_id=1, source_target_pairs={{0,9},{1,4},{2,7},{3,10},{4,1},{5,12},{6,15},{7,2},{8,13},{9,0},{1... | collective-permute-start | bytes 786440 | tf_op jit(solution)/shard_map/ppermute | solution.py:176
  42.5 0.9 %collective-permute-start.19 = (bf16[8,128,128]{2,1,0:T(8,128)(2,1)S(1)}, bf16[8,128,128]{2,1,0:T(8,128)(2,1)S(1)}, u32[]{:S(2)}, u32[]{:S(2)}) collective-permute-start(bf16[8,128,128]{2,1,0:T(8,128)(2,1)S(1)} %pad_maximum_fusion.1.refs_1_), channel_id=1, source_target_pairs={{0,9},{1,2},{2,1},{3,10},{4,7},{5,12},{6,15},{7,4},{8,11},{9,0},{1... | collective-permute-start | bytes 786440 | tf_op jit(solution)/shard_map/ppermute | solution.py:176
  43.5 0.8 %multiply_subtract_fusion = (f32[256,128]{1,0:T(8,128)}, f32[256,128]{1,0:T(8,128)}, f32[256,128]{1,0:T(8,128)}) fusion(f32[256,128]{1,0:T(8,128)S(1)} %bitcast.117, f32[256,128]{1,0:T(8,128)S(1)} %bitcast.118, f32[128,128]{1,0:T(8,128)S(1)} %get-tuple-element.40, f32[128,128]{1,0:T(8,128)S(1)} %get-tuple-element.41, f32[256,128]{1,0:T(8,128)S(1)} %bitcast.119), kind=kLoop, calls=%fused_computation.21 | loop fusion | flops 491520 | bytes 917504 | tf_op jit(solution)/shard_map/sub | solution.py:29
  44.3 1.4 %collective-permute-start.23 = (bf16[8,128,128]{2,1,0:T(8,128)(2,1)S(1)}, bf16[8,128,128]{2,1,0:T(8,128)(2,1)S(1)}, u32[]{:S(2)}, u32[]{:S(2)}) collective-permute-start(bf16[8,128,128]{2,1,0:T(8,128)(2,1)S(1)} %pad_maximum_fusion.1.refs_1_), channel_id=1, source_target_pairs={{0,1},{1,0},{2,3},{3,2},{4,5},{5,4},{6,7},{7,6},{8,9},{9,8},{10,11... | collective-permute-start | bytes 786440 | tf_op jit(solution)/shard_map/ppermute | solution.py:172
  45.6 1.7 %collective-permute-done.9.refs_0_ = bf16[8,128,128]{2,1,0:T(8,128)(2,1)S(1)} collective-permute-done((bf16[8,128,128]{2,1,0:T(8,128)(2,1)S(1)}, bf16[8,128,128]{2,1,0:T(8,128)(2,1)S(1)}, u32[]{:S(2)}, u32[]{:S(2)}) %collective-permute-start.9) | collective-permute-done | bytes 262176 | tf_op jit(solution)/shard_map/ppermute | solution.py:176
  47.8 2.4 %collective-permute-done.19.refs_0_ = bf16[8,128,128]{2,1,0:T(8,128)(2,1)S(1)} collective-permute-done((bf16[8,128,128]{2,1,0:T(8,128)(2,1)S(1)}, bf16[8,128,128]{2,1,0:T(8,128)(2,1)S(1)}, u32[]{:S(2)}, u32[]{:S(2)}) %collective-permute-start.19) | collective-permute-done | bytes 262176 | tf_op jit(solution)/shard_map/ppermute | solution.py:176
  50.2 1.2 %scatter_pieces.3.refs_2_ = bf16[8192,128]{1,0:T(8,128)(2,1)} custom-call(bf16[8,128,128]{2,1,0:T(8,128)(2,1)S(1)} %pad_maximum_fusion.refs_0_, bf16[8,128,128]{2,1,0:T(8,128)(2,1)S(1)} %pad_maximum_fusion.1.refs_1_, bf16[8,128,128]{2,1,0:T(8,128)(2,1)S(1)} %collective-permute-done.22.refs_2_, bf16[8,128,128]{2,1,0:T(8,128)(2,1)S(1)} %collective-permute-done.23.refs_3_), custom_call_target="tpu_custom_call" | custom-call | flops 1048576 | bytes 1048576 | tf_op jit(solution)/shard_map/scatter_pieces/pallas_call | solution.py:149
  51.4 0.9 %scatter_pieces.4.refs_2_ = bf16[8192,128]{1,0:T(8,128)(2,1)} custom-call(bf16[8,128,128]{2,1,0:T(8,128)(2,1)S(1)} %collective-permute-done.9.refs_0_, bf16[8,128,128]{2,1,0:T(8,128)(2,1)S(1)} %collective-permute-done.21.refs_1_, bf16[8192,128]{1,0:T(8,128)(2,1)} %scatter_pieces.3.refs_2_), custom_call_target="tpu_custom_call", output_to_operand_aliasing={{}: (2, {})} | custom-call | flops 1048576 | bytes 1048576 | tf_op jit(solution)/shard_map/scatter_pieces/pallas_call | solution.py:149
  52.4 0.9 %scatter_pieces.5 = bf16[8192,128]{1,0:T(8,128)(2,1)} custom-call(bf16[8,128,128]{2,1,0:T(8,128)(2,1)S(1)} %collective-permute-done.19.refs_0_, bf16[8,128,128]{2,1,0:T(8,128)(2,1)S(1)} %collective-permute-done.20.refs_1_, bf16[8192,128]{1,0:T(8,128)(2,1)} %scatter_pieces.4.refs_2_), custom_call_target="tpu_custom_call", output_to_operand_aliasing={{}: (2, {})} | custom-call | flops 1048576 | bytes 1048576 | tf_op jit(solution)/shard_map/scatter_pieces/pallas_call | solution.py:149
  (56 shorter events, 2.6 us)
Async XLA Ops:
  0.6 4.2 %copy-start.1 = (f32[2,16384]{1,0:T(2,128)S(1)}, f32[2,16384]{1,0:T(2,128)}, u32[]{:S(2)}) copy-start(f32[2,16384]{1,0:T(2,128)} %param.6) | copy-start | bytes 393220
  0.6 4.2 %copy-start.2 = (f32[2,16384]{1,0:T(2,128)S(1)}, f32[2,16384]{1,0:T(2,128)}, u32[]{:S(2)}) copy-start(f32[2,16384]{1,0:T(2,128)} %param.7) | copy-start | bytes 393220
  0.7 4.4 %copy-start = (f32[2,16384]{1,0:T(2,128)S(1)}, f32[2,16384]{1,0:T(2,128)}, u32[]{:S(2)}) copy-start(f32[2,16384]{1,0:T(2,128)} %param.5) | copy-start | bytes 393220
  2.2 2.8 %collective-permute-start.11 = (bf16[8,128,128]{2,1,0:T(8,128)(2,1)S(1)}, bf16[8,128,128]{2,1,0:T(8,128)(2,1)S(1)}, u32[]{:S(2)}, u32[]{:S(2)}) collective-permute-start(bf16[8,128,128]{2,1,0:T(8,128)(2,1)S(1)} %get-tuple-element.23), channel_id=1, source_target_pairs={{0,1},{1,0},{2,3},{3,2},{4,5},{5,4},{6,7},{7,6},{8,9},{9,8},{10,11... | collective-permute-start | bytes 786440 | tf_op jit(solution)/shard_map/ppermute | solution.py:172
  4.2 5.1 %collective-permute-start.10 = (bf16[8,128,128]{2,1,0:T(8,128)(2,1)S(1)}, bf16[8,128,128]{2,1,0:T(8,128)(2,1)S(1)}, u32[]{:S(2)}, u32[]{:S(2)}) collective-permute-start(bf16[8,128,128]{2,1,0:T(8,128)(2,1)S(1)} %get-tuple-element.21), channel_id=1, source_target_pairs={{0,1},{1,0},{2,3},{3,2},{4,5},{5,4},{6,7},{7,6},{8,9},{9,8},{10,11... | collective-permute-start | bytes 786440 | tf_op jit(solution)/shard_map/ppermute | solution.py:172
  4.3 5.0 %collective-permute-start = (bf16[8,128,128]{2,1,0:T(8,128)(2,1)S(1)}, bf16[8,128,128]{2,1,0:T(8,128)(2,1)S(1)}, u32[]{:S(2)}, u32[]{:S(2)}) collective-permute-start(bf16[8,128,128]{2,1,0:T(8,128)(2,1)S(1)} %get-tuple-element.17), channel_id=1, source_target_pairs={{0,1},{1,0},{2,3},{3,2},{4,5},{5,4},{6,7},{7,6},{8,9},{9,8},{10,11... | collective-permute-start | bytes 786440 | tf_op jit(solution)/shard_map/ppermute | solution.py:172
  4.8 3.0 %collective-permute-start.1 = (bf16[8,128,128]{2,1,0:T(8,128)(2,1)S(1)}, bf16[8,128,128]{2,1,0:T(8,128)(2,1)S(1)}, u32[]{:S(2)}, u32[]{:S(2)}) collective-permute-start(bf16[8,128,128]{2,1,0:T(8,128)(2,1)S(1)} %get-tuple-element.19), channel_id=1, source_target_pairs={{0,1},{1,0},{2,3},{3,2},{4,5},{5,4},{6,7},{7,6},{8,9},{9,8},{10,11... | collective-permute-start | bytes 786440 | tf_op jit(solution)/shard_map/ppermute | solution.py:172
  5.1 6.7 %collective-permute-start.12 = (bf16[8,128,128]{2,1,0:T(8,128)(2,1)S(1)}, bf16[8,128,128]{2,1,0:T(8,128)(2,1)S(1)}, u32[]{:S(2)}, u32[]{:S(2)}) collective-permute-start(bf16[8,128,128]{2,1,0:T(8,128)(2,1)S(1)} %add_convert_fusion), channel_id=1, source_target_pairs={{0,5},{1,8},{2,11},{3,6},{4,13},{5,0},{6,3},{7,14},{8,1},{9,12},{1... | collective-permute-start | bytes 786440 | tf_op jit(solution)/shard_map/ppermute | solution.py:176
  7.9 6.8 %collective-permute-start.2 = (bf16[8,128,128]{2,1,0:T(8,128)(2,1)S(1)}, bf16[8,128,128]{2,1,0:T(8,128)(2,1)S(1)}, u32[]{:S(2)}, u32[]{:S(2)}) collective-permute-start(bf16[8,128,128]{2,1,0:T(8,128)(2,1)S(1)} %add_convert_fusion.1), channel_id=1, source_target_pairs={{0,5},{1,2},{2,1},{3,6},{4,7},{5,0},{6,3},{7,4},{8,11},{9,12},{10,... | collective-permute-start | bytes 786440 | tf_op jit(solution)/shard_map/ppermute | solution.py:176
  11.9 4.8 %collective-permute-start.13 = (bf16[4,128,128]{2,1,0:T(8,128)(2,1)S(1)}, bf16[4,128,128]{2,1,0:T(8,128)(2,1)S(1)}, u32[]{:S(2)}, u32[]{:S(2)}) collective-permute-start(bf16[4,128,128]{2,1,0:T(8,128)(2,1)S(1)} %get-tuple-element.32), channel_id=1, source_target_pairs={{0,3},{1,4},{2,7},{3,0},{4,1},{5,6},{6,5},{7,2},{8,13},{9,10},{10,... | collective-permute-start | bytes 393224 | tf_op jit(solution)/shard_map/ppermute | solution.py:176
  14.8 4.5 %collective-permute-start.3 = (bf16[4,128,128]{2,1,0:T(8,128)(2,1)S(1)}, bf16[4,128,128]{2,1,0:T(8,128)(2,1)S(1)}, u32[]{:S(2)}, u32[]{:S(2)}) collective-permute-start(bf16[4,128,128]{2,1,0:T(8,128)(2,1)S(1)} %get-tuple-element.34), channel_id=1, source_target_pairs={{0,3},{1,8},{2,11},{3,0},{4,13},{5,6},{6,5},{7,14},{8,1},{9,10},{1... | collective-permute-start | bytes 393224 | tf_op jit(solution)/shard_map/ppermute | solution.py:176
  16.8 4.4 %collective-permute-start.14 = (bf16[2,128,128]{2,1,0:T(8,128)(2,1)S(1)}, bf16[2,128,128]{2,1,0:T(8,128)(2,1)S(1)}, u32[]{:S(2)}, u32[]{:S(2)}) collective-permute-start(bf16[2,128,128]{2,1,0:T(8,128)(2,1)S(1)} %get-tuple-element.36), channel_id=1, source_target_pairs={{0,9},{1,2},{2,1},{3,10},{4,7},{5,12},{6,15},{7,4},{8,11},{9,0},{1... | collective-permute-start | bytes 196616 | tf_op jit(solution)/shard_map/ppermute | solution.py:176
  19.3 4.6 %collective-permute-start.4 = (bf16[2,128,128]{2,1,0:T(8,128)(2,1)S(1)}, bf16[2,128,128]{2,1,0:T(8,128)(2,1)S(1)}, u32[]{:S(2)}, u32[]{:S(2)}) collective-permute-start(bf16[2,128,128]{2,1,0:T(8,128)(2,1)S(1)} %get-tuple-element.38), channel_id=1, source_target_pairs={{0,9},{1,4},{2,7},{3,10},{4,1},{5,12},{6,15},{7,2},{8,13},{9,0},{1... | collective-permute-start | bytes 196616 | tf_op jit(solution)/shard_map/ppermute | solution.py:176
  21.2 4.9 %collective-permute-start.15 = (bf16[1,128,128]{2,1,0:T(8,128)(2,1)S(1)}, bf16[1,128,128]{2,1,0:T(8,128)(2,1)S(1)}, u32[]{:S(2)}, u32[]{:S(2)}) collective-permute-start(bf16[1,128,128]{2,1,0:T(8,128)(2,1)S(1)} %fusion.4), channel_id=1, source_target_pairs={{0,17},{1,16},{2,19},{3,18},{4,21},{5,20},{6,23},{7,22},{8,25},{9,... | collective-permute-start | bytes 98312 | tf_op jit(solution)/shard_map/ppermute | solution.py:176
  23.9 4.5 %collective-permute-start.5 = (bf16[1,128,128]{2,1,0:T(8,128)(2,1)S(1)}, bf16[1,128,128]{2,1,0:T(8,128)(2,1)S(1)}, u32[]{:S(2)}, u32[]{:S(2)}) collective-permute-start(bf16[1,128,128]{2,1,0:T(8,128)(2,1)S(1)} %fusion.6), channel_id=1, source_target_pairs={{0,17},{1,16},{2,19},{3,18},{4,21},{5,20},{6,23},{7,22},{8,25},{9,... | collective-permute-start | bytes 98312 | tf_op jit(solution)/shard_map/ppermute | solution.py:176
  26.1 5.0 %collective-permute-start.16 = (bf16[1,128,128]{2,1,0:T(8,128)(2,1)S(1)}, bf16[1,128,128]{2,1,0:T(8,128)(2,1)S(1)}, u32[]{:S(2)}, u32[]{:S(2)}) collective-permute-start(bf16[1,128,128]{2,1,0:T(8,128)(2,1)S(1)} %get-tuple-element.39), channel_id=1, source_target_pairs={{0,17},{1,16},{2,19},{3,18},{4,21},{5,20},{6,23},{7,22},{8,25},{9,... | collective-permute-start | bytes 98312 | tf_op jit(solution)/shard_map/ppermute | solution.py:176
  28.5 4.5 %collective-permute-start.6 = (bf16[1,128,128]{2,1,0:T(8,128)(2,1)S(1)}, bf16[1,128,128]{2,1,0:T(8,128)(2,1)S(1)}, u32[]{:S(2)}, u32[]{:S(2)}) collective-permute-start(bf16[1,128,128]{2,1,0:T(8,128)(2,1)S(1)} %get-tuple-element.42), channel_id=1, source_target_pairs={{0,17},{1,16},{2,19},{3,18},{4,21},{5,20},{6,23},{7,22},{8,25},{9,... | collective-permute-start | bytes 98312 | tf_op jit(solution)/shard_map/ppermute | solution.py:176
  31.1 4.2 %collective-permute-start.17 = (bf16[2,128,128]{2,1,0:T(8,128)(2,1)S(1)}, bf16[2,128,128]{2,1,0:T(8,128)(2,1)S(1)}, u32[]{:S(2)}, u32[]{:S(2)}) collective-permute-start(bf16[2,128,128]{2,1,0:T(8,128)(2,1)S(1)} %pad_maximum_fusion.6), channel_id=1, source_target_pairs={{0,5},{1,4},{2,7},{3,6},{4,1},{5,0},{6,3},{7,2},{8,13},{9,12},{10,... | collective-permute-start | bytes 196616 | tf_op jit(solution)/shard_map/ppermute | solution.py:176
  33.1 3.9 %collective-permute-start.7 = (bf16[2,128,128]{2,1,0:T(8,128)(2,1)S(1)}, bf16[2,128,128]{2,1,0:T(8,128)(2,1)S(1)}, u32[]{:S(2)}, u32[]{:S(2)}) collective-permute-start(bf16[2,128,128]{2,1,0:T(8,128)(2,1)S(1)} %pad_maximum_fusion.5), channel_id=1, source_target_pairs={{0,5},{1,2},{2,1},{3,6},{4,7},{5,0},{6,3},{7,4},{8,11},{9,12},{10,... | collective-permute-start | bytes 196616 | tf_op jit(solution)/shard_map/ppermute | solution.py:176
  35.3 7.2 %collective-permute-start.18 = (bf16[4,128,128]{2,1,0:T(8,128)(2,1)S(1)}, bf16[4,128,128]{2,1,0:T(8,128)(2,1)S(1)}, u32[]{:S(2)}, u32[]{:S(2)}) collective-permute-start(bf16[4,128,128]{2,1,0:T(8,128)(2,1)S(1)} %pad_maximum_fusion.4), channel_id=1, source_target_pairs={{0,3},{1,8},{2,11},{3,0},{4,13},{5,6},{6,5},{7,14},{8,1},{9,10},{1... | collective-permute-start | bytes 393224 | tf_op jit(solution)/shard_map/ppermute | solution.py:176
  37.0 4.5 %collective-permute-start.8 = (bf16[4,128,128]{2,1,0:T(8,128)(2,1)S(1)}, bf16[4,128,128]{2,1,0:T(8,128)(2,1)S(1)}, u32[]{:S(2)}, u32[]{:S(2)}) collective-permute-start(bf16[4,128,128]{2,1,0:T(8,128)(2,1)S(1)} %pad_maximum_fusion.2), channel_id=1, source_target_pairs={{0,3},{1,8},{2,11},{3,0},{4,13},{5,6},{6,5},{7,14},{8,1},{9,10},{1... | collective-permute-start | bytes 393224 | tf_op jit(solution)/shard_map/ppermute | solution.py:176
  41.5 5.9 %collective-permute-start.9 = (bf16[8,128,128]{2,1,0:T(8,128)(2,1)S(1)}, bf16[8,128,128]{2,1,0:T(8,128)(2,1)S(1)}, u32[]{:S(2)}, u32[]{:S(2)}) collective-permute-start(bf16[8,128,128]{2,1,0:T(8,128)(2,1)S(1)} %pad_maximum_fusion.refs_0_), channel_id=1, source_target_pairs={{0,9},{1,4},{2,7},{3,10},{4,1},{5,12},{6,15},{7,2},{8,13},{9,0},{1... | collective-permute-start | bytes 786440 | tf_op jit(solution)/shard_map/ppermute | solution.py:176
  42.5 7.6 %collective-permute-start.19 = (bf16[8,128,128]{2,1,0:T(8,128)(2,1)S(1)}, bf16[8,128,128]{2,1,0:T(8,128)(2,1)S(1)}, u32[]{:S(2)}, u32[]{:S(2)}) collective-permute-start(bf16[8,128,128]{2,1,0:T(8,128)(2,1)S(1)} %pad_maximum_fusion.1.refs_1_), channel_id=1, source_target_pairs={{0,9},{1,2},{2,1},{3,10},{4,7},{5,12},{6,15},{7,4},{8,11},{9,0},{1... | collective-permute-start | bytes 786440 | tf_op jit(solution)/shard_map/ppermute | solution.py:176
  44.3 5.9 %collective-permute-start.23 = (bf16[8,128,128]{2,1,0:T(8,128)(2,1)S(1)}, bf16[8,128,128]{2,1,0:T(8,128)(2,1)S(1)}, u32[]{:S(2)}, u32[]{:S(2)}) collective-permute-start(bf16[8,128,128]{2,1,0:T(8,128)(2,1)S(1)} %pad_maximum_fusion.1.refs_1_), channel_id=1, source_target_pairs={{0,1},{1,0},{2,3},{3,2},{4,5},{5,4},{6,7},{7,6},{8,9},{9,8},{10,11... | collective-permute-start | bytes 786440 | tf_op jit(solution)/shard_map/ppermute | solution.py:172
  45.6 4.5 %collective-permute-start.22 = (bf16[8,128,128]{2,1,0:T(8,128)(2,1)S(1)}, bf16[8,128,128]{2,1,0:T(8,128)(2,1)S(1)}, u32[]{:S(2)}, u32[]{:S(2)}) collective-permute-start(bf16[8,128,128]{2,1,0:T(8,128)(2,1)S(1)} %pad_maximum_fusion.refs_0_), channel_id=1, source_target_pairs={{0,1},{1,0},{2,3},{3,2},{4,5},{5,4},{6,7},{7,6},{8,9},{9,8},{10,11... | collective-permute-start | bytes 786440 | tf_op jit(solution)/shard_map/ppermute | solution.py:172
  47.4 4.1 %collective-permute-start.21 = (bf16[8,128,128]{2,1,0:T(8,128)(2,1)S(1)}, bf16[8,128,128]{2,1,0:T(8,128)(2,1)S(1)}, u32[]{:S(2)}, u32[]{:S(2)}) collective-permute-start(bf16[8,128,128]{2,1,0:T(8,128)(2,1)S(1)} %collective-permute-done.9.refs_0_), channel_id=1, source_target_pairs={{0,1},{1,0},{2,3},{3,2},{4,5},{5,4},{6,7},{7,6},{8,9},{9,8},{10,11... | collective-permute-start | bytes 786440 | tf_op jit(solution)/shard_map/ppermute | solution.py:172
  50.2 2.2 %collective-permute-start.20 = (bf16[8,128,128]{2,1,0:T(8,128)(2,1)S(1)}, bf16[8,128,128]{2,1,0:T(8,128)(2,1)S(1)}, u32[]{:S(2)}, u32[]{:S(2)}) collective-permute-start(bf16[8,128,128]{2,1,0:T(8,128)(2,1)S(1)} %collective-permute-done.19.refs_0_), channel_id=1, source_target_pairs={{0,1},{1,0},{2,3},{3,2},{4,5},{5,4},{6,7},{7,6},{8,9},{9,8},{10,11... | collective-permute-start | bytes 786440 | tf_op jit(solution)/shard_map/ppermute | solution.py:172
